TPU v7x, 32 devices: a whole 2x2x4 slice. The times are simulated.
32 devices in a mesh: grp: 2 (over y), dp: 16 (over z, x, core).
Axes of the slice: x: 2, y: 2, z: 4, core: 2. Of those that a mesh axis runs over, the one named last changes fastest.
Arguments:
- hidden_in: bfloat16 [2, 64, 4096], P(None, ('grp', 'dp')), parts along dimension 1, may hold values from -6 to 6
- norm_gain: float32 [4096], replicated, may hold values from 0.1 to 1.9
- queries: bfloat16 [2, 64, 4096], P(None, ('grp', 'dp')), parts along dimension 1, may hold values from -72 to 72
- new_keys: bfloat16 [2, 64, 1024], P(None, ('grp', 'dp')), parts along dimension 1, may hold values from -9 to 9
- new_values: bfloat16 [2, 64, 1024], P(None, ('grp', 'dp')), parts along dimension 1, may hold values from -6 to 6
- cache_keys: bfloat16 [64, 384, 1024], P(('grp', 'dp')), parts along dimension 0, may hold values from -9 to 9
- cache_values: bfloat16 [64, 384, 1024], P(('grp', 'dp')), parts along dimension 0, may hold values from -6 to 6
- lengths: int32 [64], P(('grp', 'dp')), parts along dimension 0, may hold values from 1 to 384
- routes: int32 [2, 64, 2], P(None, ('grp', 'dp')), parts along dimension 1, may hold values from 0 to 3, all different within a row; in each aligned block of 2 rows (0 to 1, 2 to 3, ..., all dimensions but the last counted through in order) at most 2 rows name the same one
- gate_logits: float32 [2, 64, 2], P(None, ('grp', 'dp')), parts along dimension 1, may hold values from -6 to 6
- w_gate: bfloat16 [28672, 4096], P('dp'), may hold values from -0.09375 to 0.09375
- w_up: bfloat16 [28672, 4096], P('dp'), may hold values from -0.09375 to 0.09375
- w_down: bfloat16 [28672, 4096], P('dp'), may hold values from -0.0625 to 0.0625
Outputs:
- hidden_out: bfloat16 [2, 64, 4096], P(None, ('grp', 'dp')), parts along dimension 1
There are 2 independent parts, one for each index of `grp`. A program takes and returns all parts, laid end to end along the dimension named above; an argument that names none is the same for every part. Nothing has to cross between parts.
Inputs may be any that keep to these rules, and one draw needn't show every extreme that they name: `routes`: each token names 2 different experts. Among the 2 tokens of one device at one decoded position no expert is named more than 2 times, a bound that some block reaches.
All inputs are finite; a program needn't handle non-finite values.
Results may differ from a plain program's by a relative error of at most 0.0055.
Values may be sent and summed in bfloat16 or wider, within the bound.
A program may use at most 192 MiB of HBM per device.

v0:
```python
import jax
import jax.numpy as jnp
from jax import lax
from jax.sharding import PartitionSpec as P

HEADS = 32
KV_HEADS = 8
HEAD_DIM = 128
TOP = 2
EXPERTS = 4
NEW = 2
CAP = 2


def attend(queries, new_keys, new_values, cache_keys, cache_values, lengths):
    docs = queries.shape[1]
    cache_len = cache_keys.shape[1]
    group_size = HEADS // KV_HEADS
    score_scale = HEAD_DIM ** (-0.5)
    query_heads = queries.reshape(NEW, docs, KV_HEADS, group_size, HEAD_DIM)
    keys_cache = cache_keys.reshape(docs, cache_len, KV_HEADS, HEAD_DIM)
    vals_cache = cache_values.reshape(docs, cache_len, KV_HEADS, HEAD_DIM)
    keys_fresh = new_keys.reshape(NEW, docs, KV_HEADS, HEAD_DIM)
    vals_fresh = new_values.reshape(NEW, docs, KV_HEADS, HEAD_DIM)
    scores_cache = (
        jnp.einsum("tdhgc,dshc->tdhgs", query_heads, keys_cache, preferred_element_type=jnp.float32)
        * score_scale
    )
    scores_fresh = (
        jnp.einsum("tdhgc,udhc->tdhgu", query_heads, keys_fresh, preferred_element_type=jnp.float32)
        * score_scale
    )
    positions = jnp.arange(cache_len, dtype=jnp.int32)
    in_range = positions[None, :] < lengths[:, None]
    scores_cache = jnp.where(in_range[None, :, None, None, :], scores_cache, -1e30)
    order = jnp.arange(NEW, dtype=jnp.int32)
    causal = order[None, :] <= order[:, None]
    scores_fresh = jnp.where(causal[:, None, None, None, :], scores_fresh, -1e30)
    largest = jnp.maximum(
        jnp.max(scores_cache, -1, keepdims=True), jnp.max(scores_fresh, -1, keepdims=True)
    )
    exp_cache = jnp.exp(scores_cache - largest)
    exp_fresh = jnp.exp(scores_fresh - largest)
    total = jnp.sum(exp_cache, -1, keepdims=True) + jnp.sum(exp_fresh, -1, keepdims=True)
    probs_cache = (exp_cache / total).astype(jnp.bfloat16)
    probs_fresh = (exp_fresh / total).astype(jnp.bfloat16)
    context = jnp.einsum(
        "tdhgs,dshc->tdhgc", probs_cache, vals_cache, preferred_element_type=jnp.float32
    )
    context = context + jnp.einsum(
        "tdhgu,udhc->tdhgc", probs_fresh, vals_fresh, preferred_element_type=jnp.float32
    )
    return context.reshape(NEW, docs, HEADS * HEAD_DIM)


def slot_table(route_rows):
    flat_ids = route_rows.reshape(-1)
    matches = (flat_ids[:, None] == jnp.arange(EXPERTS, dtype=jnp.int32)[None, :]).astype(jnp.int32)
    before = jnp.cumsum(matches, axis=0) - matches
    slot_ids = flat_ids * CAP + jnp.sum(before * matches, axis=1)
    slots_all = jnp.arange(EXPERTS * CAP, dtype=jnp.int32)
    return (slots_all[:, None] == slot_ids[None, :]).astype(jnp.float32)


def expert_rows(flat_rows, w_gate, w_up, w_down):
    gate_val = lax.dot_general(
        flat_rows, w_gate, (((1,), (1,)), ((), ())), preferred_element_type=jnp.float32
    )
    up_val = lax.dot_general(
        flat_rows, w_up, (((1,), (1,)), ((), ())), preferred_element_type=jnp.float32
    )
    act = (jax.nn.silu(gate_val) * up_val).astype(jnp.bfloat16)
    return jnp.dot(act, w_down, preferred_element_type=jnp.float32)


def per_device(
    hidden_in,
    norm_gain,
    queries,
    new_keys,
    new_values,
    cache_keys,
    cache_values,
    lengths,
    routes,
    gate_logits,
    w_gate,
    w_up,
    w_down,
):
    docs = hidden_in.shape[1]
    width = hidden_in.shape[2]
    context = attend(queries, new_keys, new_values, cache_keys, cache_values, lengths)
    carried = hidden_in.astype(jnp.float32) + context
    normed = (
        carried * lax.rsqrt(jnp.mean(carried * carried, -1, keepdims=True) + 1e-05) * norm_gain
    ).astype(jnp.bfloat16)
    groups = lax.axis_size("dp") // EXPERTS
    top_share = jax.nn.sigmoid(gate_logits[..., 0] - gate_logits[..., 1])
    shares = jnp.stack([top_share, 1.0 - top_share], axis=-1)
    tables = [slot_table(routes[position]) for position in range(NEW)]
    send_list = []
    for position in range(NEW):
        copies = jnp.repeat(normed[position], TOP, axis=0)
        packed = jnp.dot(
            tables[position].astype(jnp.bfloat16), copies, preferred_element_type=jnp.float32
        )
        packed = packed.astype(jnp.bfloat16).reshape(EXPERTS, CAP, width)
        send_list.append(jnp.repeat(packed, groups, axis=0))
    payload = jnp.concatenate(send_list, axis=1)
    slots = payload.shape[1]
    arrivals = lax.all_to_all(payload, "dp", split_axis=0, concat_axis=0, tiled=True)
    senders, serve_slots, features = arrivals.shape
    partial_value = expert_rows(
        arrivals.reshape(senders * serve_slots, features), w_gate, w_up, w_down
    ).reshape(senders, serve_slots, features)
    back = lax.all_to_all(
        partial_value.astype(jnp.bfloat16), "dp", split_axis=0, concat_axis=0, tiled=True
    ).astype(partial_value.dtype)
    summed_all = jnp.sum(back.reshape(EXPERTS, groups, slots, width), axis=1)
    back_list = [summed_all[:, position * CAP : (position + 1) * CAP] for position in range(NEW)]
    results = []
    for position in range(NEW):
        summed = back_list[position].reshape(EXPERTS * CAP, width)
        per_route = jnp.dot(
            tables[position].T,
            summed,
            precision=lax.Precision.HIGHEST,
            preferred_element_type=jnp.float32,
        )
        per_route = per_route.reshape(docs, TOP, width)
        results.append(
            carried[position] + jnp.sum(shares[position][:, :, None] * per_route, axis=1)
        )
    return jnp.stack(results, axis=0).astype(jnp.bfloat16)


def solution(mesh):
    in_specs = (
        P(None, ("grp", "dp"), None),
        P(),
        P(None, ("grp", "dp"), None),
        P(None, ("grp", "dp"), None),
        P(None, ("grp", "dp"), None),
        P(("grp", "dp"), None, None),
        P(("grp", "dp"), None, None),
        P(("grp", "dp")),
        P(None, ("grp", "dp"), None),
        P(None, ("grp", "dp"), None),
        P("dp", None),
        P("dp", None),
        P("dp", None),
    )
    out_specs = P(None, ("grp", "dp"), None)
    return jax.shard_map(
        per_device, mesh=mesh, in_specs=in_specs, out_specs=out_specs, check_vma=False
    )
```

profile of v0, /device:TPU:0, one launch (start us, length us, event | category | flops | bytes accessed | tf_op | source)
XLA Modules:
  0.0 75.4 jit_solution(16364766368387052277)
XLA Ops:
  0.0 0.8 %reshape.178 = bf16[2,2,8,4,128]{4,3,2,1,0:T(4,128)(2,1)S(1)} reshape(bf16[2,2,4096]{2,1,0:T(2,128)(2,1)} %param.15) | data formatting | bytes 65536 | tf_op jit(solution)/shard_map/reshape | solution.py:20
  0.8 1.8 %copy.46 = bf16[96,8,8,128]{3,2,1,0:T(8,128)(2,1)S(1)} copy(bf16[96,8,8,128]{3,1,2,0:T(8,128)(2,1)} %bitcast.56) | data formatting | bytes 3145728
  2.7 0.0 copy-start.7
  2.7 0.0 copy-start.3
  2.7 0.1 bitcast_bitcast_fusion.1
  2.8 0.5 copy-done.7
  3.3 0.1 iota_compare_fusion.2
  3.4 0.0 copy-done.3
  3.4 0.0 copy-start.4
  3.4 0.0 copy-start
  3.4 0.8 %fusion.51 = (f32[2,2,8,4]{3,0,2,1:T(2,128)S(1)}, f32[2,2,8,4,384]{4,3,0,2,1:T(4,128)S(1)}) fusion(bf16[2,2,8,4,128]{4,3,2,1,0:T(4,128)(2,1)S(1)} %reshape.178, bf16[2,384,8,128,1]{3,2,1,0,4:T(8,128)(2,1)S(1)} %bitcast_bitcast_fusion.1, pred[2,384]{1,0:T(4,128)(4,1)S(1)} %iota_compare_fusion.2), kind=kOutput, calls=%fused_computation.84 | convolution fusion | flops 12730240 | bytes 1803520 | tf_op jit(solution)/shard_map/tdhgc,dshc->tdhgs/dot_general | solution.py:26
  4.2 0.4 fusion.52
  4.6 0.1 fusion.37
  4.7 0.2 fusion.30
  4.9 0.0 copy-done.4
  5.0 0.0 copy-done
  5.0 0.4 copy.47
  5.4 0.1 bitcast_bitcast_fusion
  5.6 0.2 fusion.38
  5.8 0.0 copy-start.1
  5.8 0.0 copy-start.2
  5.8 0.0 copy-start.6
  5.8 0.5 fusion.17
  6.3 0.1 reshape.182
  6.4 0.2 copy-done.1
  6.5 0.1 multiply_reduce_fusion
  6.7 0.0 copy-done.2
  6.7 0.1 multiply_convert_fusion
  6.9 0.0 copy-done.6
  6.9 0.1 reshape_squeeze.6
  7.0 0.1 fusion.44
  7.1 0.2 select_reduce_fusion.1
  7.3 0.1 convolution_convert_fusion.2
  7.4 0.1 reshape.184
  7.6 0.1 reshape_squeeze.7
  7.7 0.1 fusion.42
  7.8 0.2 select_reduce_fusion
  8.0 0.1 convolution_convert_fusion.1
  8.1 0.1 reshape.187
  8.2 0.2 broadcast_in_dim.37
  8.4 0.2 broadcast_in_dim.61
  8.6 0.5 pad_maximum_fusion
  9.1 21.5 %all_to_all.10 = bf16[16,4,4096]{2,1,0:T(4,128)(2,1)S(1)} all-to-all(bf16[16,4,4096]{2,1,0:T(4,128)(2,1)S(1)} %pad_maximum_fusion), channel_id=1, replica_groups=mesh['grp'=2,'dp'=16] {'dp'}, dimensions={0} | all-to-all | bytes 1048576 | tf_op jit(solution)/shard_map/all_to_all | solution.py:112
  30.6 0.1 reshape.189
  30.7 9.7 %fusion.53 = f32[64,1792]{1,0:T(8,128)S(1)} fusion(bf16[64,4096]{1,0:T(8,128)(2,1)S(1)} %reshape.189, bf16[1792,4096]{1,0:T(8,128)(2,1)} %param.23), kind=kOutput, calls=%fused_computation.86 | convolution fusion | flops 939524096 | bytes 15663104 | tf_op jit(solution)/shard_map/dot_general | solution.py:66
  40.4 13.5 %convolution_convert_fusion = bf16[64,4096]{1,0:T(8,128)(2,1)S(1)} fusion(bf16[1792,4096]{1,0:T(8,128)(2,1)} %param.25, bf16[64,4096]{1,0:T(8,128)(2,1)S(1)} %reshape.189, bf16[1792,4096]{1,0:T(8,128)(2,1)} %param.24, f32[64,1792]{1,0:T(8,128)S(1)} %fusion.53), kind=kOutput, calls=%fused_computation | convolution fusion | flops 1879998464 | bytes 30867456 | tf_op jit(solution)/shard_map/dot_general | solution.py:73
  54.0 0.0 copy-start.5
  54.0 1.0 %convert_element_type.61 = bf16[16,4,4096]{2,1,0:T(4,128)(2,1)} reshape(bf16[64,4096]{1,0:T(8,128)(2,1)S(1)} %convolution_convert_fusion) | data formatting | bytes 1048576 | tf_op jit(solution)/shard_map/convert_element_type | solution.py:118
  55.0 4.2 %all-to-all-start.1 = ((bf16[16,4,4096]{2,1,0:T(4,128)(2,1)}), bf16[16,4,4096]{2,1,0:T(4,128)(2,1)S(1)}, u32[]{:S(2)}, u32[]{:S(2)}) async-start(bf16[16,4,4096]{2,1,0:T(4,128)(2,1)} %convert_element_type.61), calls=%async_computation.1 | async-start | bytes 1048576 | tf_op jit(solution)/shard_map/all_to_all | solution.py:117
  59.2 0.1 iota_compare_fusion.3
  59.3 0.1 iota_compare_fusion.6
  59.4 0.0 copy-done.5
  59.4 0.1 broadcast_subtract_fusion
  59.4 0.1 fusion.46
  59.5 13.9 %all-to-all-done.1 = bf16[16,4,4096]{2,1,0:T(4,128)(2,1)S(1)} async-done(((bf16[16,4,4096]{2,1,0:T(4,128)(2,1)}), bf16[16,4,4096]{2,1,0:T(4,128)(2,1)S(1)}, u32[]{:S(2)}, u32[]{:S(2)}) %all-to-all-start.1) | async-done | bytes 524320 | tf_op jit(solution)/shard_map/all_to_all | solution.py:117
  73.4 0.3 convert_reduce_fusion
  73.7 0.1 fusion.49
  73.8 0.1 reshape.201
  73.9 0.1 reshape.200
  74.0 0.3 fusion.21
  74.3 0.3 fusion.20
  74.7 0.7 pad_maximum_fusion.1
  (20 shorter events, 0.4 us)
Async XLA Ops:
  2.7 0.7 copy-start.7
  2.7 0.7 copy-start.3
  3.4 1.5 %copy-start.4 = (bf16[2,2,1024]{2,1,0:T(2,128)(2,1)S(1)}, bf16[2,2,1024]{2,1,0:T(2,128)(2,1)}, u32[]{:S(2)}) copy-start(bf16[2,2,1024]{2,1,0:T(2,128)(2,1)} %param.17) | copy-start | bytes 24580
  3.4 1.6 %copy-start = (bf16[2,384,1024]{2,1,0:T(8,128)(2,1)S(1)}, bf16[2,384,1024]{2,1,0:T(8,128)(2,1)}, u32[]{:S(2)}) copy-start(bf16[2,384,1024]{2,1,0:T(8,128)(2,1)} %param.19) | copy-start | bytes 4718596
  5.8 0.8 %copy-start.1 = (bf16[2,2,4096]{2,1,0:T(2,128)(2,1)S(1)}, bf16[2,2,4096]{2,1,0:T(2,128)(2,1)}, u32[]{:S(2)}) copy-start(bf16[2,2,4096]{2,1,0:T(2,128)(2,1)} %param.13) | copy-start | bytes 98308
  5.8 0.9 %copy-start.2 = (f32[4096]{0:T(1024)S(1)}, f32[4096]{0:T(1024)}, u32[]{:S(2)}) copy-start(f32[4096]{0:T(1024)} %param.14) | copy-start | bytes 49156
  5.8 1.1 %copy-start.6 = (s32[2,2,2]{2,1,0:T(2,128)S(1)}, s32[2,2,2]{2,1,0:T(2,128)}, u32[]{:S(2)}) copy-start(s32[2,2,2]{2,1,0:T(2,128)} %param.21) | copy-start | bytes 100
  54.0 5.4 %copy-start.5 = (f32[2,2,2]{2,1,0:T(2,128)S(1)}, f32[2,2,2]{2,1,0:T(2,128)}, u32[]{:S(2)}) copy-start(f32[2,2,2]{2,1,0:T(2,128)} %param.22) | copy-start | bytes 100
  55.0 18.4 %all-to-all-start.1 = ((bf16[16,4,4096]{2,1,0:T(4,128)(2,1)}), bf16[16,4,4096]{2,1,0:T(4,128)(2,1)S(1)}, u32[]{:S(2)}, u32[]{:S(2)}) async-start(bf16[16,4,4096]{2,1,0:T(4,128)(2,1)} %convert_element_type.61), calls=%async_computation.1 | async-start | bytes 1048576 | tf_op jit(solution)/shard_map/all_to_all | solution.py:117
where the time goes:
time: 75.9 us; the launch traced here: 75.4 us
  matrix products  26.1 us (34%)
  blocking collectives  21.5 us (28%)
  waiting for transfers between devices  13.9 us (18%)
  local copies, waits for them, and re-layouts  6.33 us (8%)
  starting transfers between devices  4.17 us (5%)
  other arithmetic  3.07 us (4%)
    all_to_all x1, blocking collectives, per_device(): lax.all_to_all(payload, 'dp', split_axis=0, concat_axis=0, tiled=True)  21.5 us
    all_to_all x1, waiting for transfers between devices, per_device(): lax.all_to_all(partial_value.astype(jnp.bfloat16), 'dp', split_axis=0, co...  13.9 us
    dot_general x1, matrix products, expert_rows(): return jnp.dot(act, w_down, preferred_element_type=jnp.float32)  13.5 us
    dot_general x1, matrix products, expert_rows(): lax.dot_general(flat_rows, w_gate, (((1,), (1,)), ((), ())), preferred_el...  9.72 us
    all_to_all x1, starting transfers between devices, per_device(): lax.all_to_all(partial_value.astype(jnp.bfloat16), 'dp', split_axis=0, co...  4.17 us
    unnamed x18, local copies, waits for them, and re-layouts  3.02 us
  transfers between devices with their start and end apart: 1, of which 1 were waited for; matrix products, arithmetic and copies ran while one was open for 0% of the time, Pallas kernels for 0%

commit v1 on v0

v1 whole, which is shorter than its diff:
```python
import functools

import jax
import jax.numpy as jnp
from jax import lax
from jax.experimental import pallas as pl
from jax.experimental.pallas import tpu as pltpu
from jax.sharding import PartitionSpec as P

HEAD_DIM = 128
EXPERTS = 4
MESH = pl.DeviceIdType.MESH
F32 = jnp.float32
BF16 = jnp.bfloat16


def kernel(
    n,
    hc,
    cw,
    lengths_ref,
    routes_ref,
    logits_ref,
    hidden_ref,
    gain_ref,
    q_ref,
    nk_ref,
    nv_ref,
    ck_hbm,
    cv_hbm,
    wg_hbm,
    wu_hbm,
    wd_hbm,
    out_ref,
    kbuf,
    vbuf,
    wg,
    wu,
    wd,
    qs,
    ctx,
    carried,
    blocks,
    xs,
    xb,
    act,
    part,
    s1,
    r1,
    s2,
    r2,
    s3,
    r3,
    sem_kv,
    sem_gu,
    sem_d,
    sem_a,
    sem_b,
    sem_c,
    sem_1,
    sem_2,
    sem_3,
):
    new, docs, width = hidden_ref.shape
    tokens = new * docs
    cache_len, kv_width = ck_hbm.shape[1], ck_hbm.shape[2]
    kv_heads = kv_width // HEAD_DIM
    group = width // kv_width
    rows8 = new * group
    hidden = wg_hbm.shape[0]
    nj = hidden // hc
    nk = width // cw
    quads = n // 4
    rows = n * tokens
    score_scale = HEAD_DIM ** (-0.5)

    grp, me = lax.axis_index("grp"), lax.axis_index("dp")
    core = lax.rem(me, 2)
    xbit = lax.rem(me // 2, 2)
    quad = me // 4
    core_dev = (grp, me + 1 - 2 * core)
    x_dev = (grp, me + 2 - 4 * xbit)

    def quad_dev(d):
        return (grp, lax.rem(quad + d, quads) * 4 + lax.rem(me, 4))

    barrier = pltpu.get_barrier_semaphore()
    for dev in [core_dev, x_dev] + [quad_dev(d) for d in range(1, quads)]:
        pl.semaphore_signal(barrier, inc=1, device_id=dev, device_id_type=MESH)

    k_copies = [
        pltpu.make_async_copy(ck_hbm.at[d], kbuf.at[d], sem_kv.at[0, d]) for d in range(docs)
    ]
    v_copies = [
        pltpu.make_async_copy(cv_hbm.at[d], vbuf.at[d], sem_kv.at[1, d]) for d in range(docs)
    ]
    for copy in k_copies + v_copies:
        copy.start()

    def gate_copy(j):
        return pltpu.make_async_copy(wg_hbm.at[pl.ds(j * hc, hc)], wg.at[j], sem_gu.at[0, j])

    def up_copy(j):
        return pltpu.make_async_copy(wu_hbm.at[pl.ds(j * hc, hc)], wu.at[j], sem_gu.at[1, j])

    def down_copy(k):
        return pltpu.make_async_copy(wd_hbm.at[:, pl.ds(k * cw, cw)], wd.at[k], sem_d.at[k])

    for j in range(nj):
        gate_copy(j).start()
        up_copy(j).start()
    for k in range(nk):
        down_copy(k).start()

    for t in range(new):
        q32 = q_ref[t].astype(F32)
        for d in range(docs):
            for head in range(kv_heads * group):
                h, g = head // group, head % group
                r = t * group + g
                qs[d * kv_heads + h, r : r + 1, :] = q32[
                    d : d + 1, head * HEAD_DIM : (head + 1) * HEAD_DIM
                ]
    nk32 = [nk_ref[u].astype(F32) for u in range(new)]
    nv32 = [nv_ref[u].astype(F32) for u in range(new)]
    row_pos = lax.broadcasted_iota(jnp.int32, (rows8, 1), 0) // group
    col = lax.broadcasted_iota(jnp.int32, (rows8, cache_len), 1)
    for d in range(docs):
        k_copies[d].wait()
        v_copies[d].wait()
        keep = col < lengths_ref[d]
        for h in range(kv_heads):
            lanes = slice(h * HEAD_DIM, (h + 1) * HEAD_DIM)
            q8 = qs[d * kv_heads + h]
            scores = lax.dot_general(
                q8.astype(BF16),
                kbuf[d, :, lanes],
                (((1,), (1,)), ((), ())),
                preferred_element_type=F32,
            )
            scores = jnp.where(keep, scores * score_scale, -1e30)
            fresh = []
            for u in range(new):
                s = jnp.sum(q8 * nk32[u][d : d + 1, lanes], axis=1, keepdims=True) * score_scale
                fresh.append(jnp.where(row_pos >= u, s, -1e30))
            largest = jnp.max(scores, axis=1, keepdims=True)
            for s in fresh:
                largest = jnp.maximum(largest, s)
            e = jnp.exp(scores - largest)
            ef = [jnp.exp(s - largest) for s in fresh]
            total = jnp.sum(e, axis=1, keepdims=True)
            for x in ef:
                total = total + x
            c8 = jnp.dot(
                (e / total).astype(BF16), vbuf[d, :, lanes], preferred_element_type=F32
            )
            for u in range(new):
                c8 = c8 + (ef[u] / total).astype(BF16).astype(F32) * nv32[u][d : d + 1, lanes]
            for t in range(new):
                for g in range(group):
                    r = t * group + g
                    head = h * group + g
                    ctx[t * docs + d : t * docs + d + 1, head * HEAD_DIM : (head + 1) * HEAD_DIM] = c8[
                        r : r + 1
                    ]
    for t in range(new):
        carried[t * docs : (t + 1) * docs, :] = (
            hidden_ref[t].astype(F32) + ctx[t * docs : (t + 1) * docs, :]
        )
    car = carried[...]
    mean = jnp.mean(car * car, axis=1, keepdims=True)
    blocks[me] = (car * lax.rsqrt(mean + 1e-05) * gain_ref[...]).astype(BF16)

    pl.semaphore_wait(barrier, quads + 1)

    def block_copy(index, send_sem, recv_sem, dev):
        return pltpu.make_async_remote_copy(
            src_ref=blocks.at[index],
            dst_ref=blocks.at[index],
            send_sem=send_sem,
            recv_sem=recv_sem,
            device_id=dev,
            device_id_type=MESH,
        )

    inner = lax.rem(me, 4)

    def place(d, y, c):
        return lax.rem(quad + quads - d, quads) * 4 + lax.rem(xbit + y, 2) * 2 + lax.rem(core + c, 2)

    out_a = [
        block_copy(me, sem_a.at[0, d], sem_a.at[1, d], quad_dev(d)) for d in range(1, quads)
    ]
    out_b = [
        block_copy(place(d, 0, 0), sem_b.at[0, d], sem_b.at[1, d], x_dev) for d in range(quads)
    ]
    out_c = [
        [
            block_copy(place(d, y, 0), sem_c.at[0, y, d], sem_c.at[1, y, d], core_dev)
            for y in range(2)
        ]
        for d in range(quads)
    ]
    in_a = [None] + [
        block_copy(place(d, 0, 0), sem_a.at[0, d], sem_a.at[1, d], core_dev)
        for d in range(1, quads)
    ]
    in_b = [
        block_copy(place(d, 1, 0), sem_b.at[0, d], sem_b.at[1, d], x_dev) for d in range(quads)
    ]
    in_c = [
        [
            block_copy(place(d, y, 1), sem_c.at[0, y, d], sem_c.at[1, y, d], core_dev)
            for y in range(2)
        ]
        for d in range(quads)
    ]
    for copy in out_a:
        copy.start()
    order = [0] + [d for i in range(1, quads // 2 + 1) for d in dict.fromkeys([i, quads - i])]
    for d in order:
        if d > 0:
            in_a[d].wait_recv()
        out_b[d].start()
        out_c[d][0].start()
    for d in order:
        in_b[d].wait_recv()
        out_c[d][1].start()
    for d in order:
        for y in range(2):
            in_c[d][y].wait_recv()
    for b in range(n):
        xs[b * tokens : (b + 1) * tokens, :] = blocks[b].astype(F32)
    xb[...] = xs[...].astype(BF16)

    def hidden_step(j):
        gate_copy(j).wait()
        up_copy(j).wait()
        x = xb[...]
        dims = (((1,), (1,)), ((), ()))
        gate = lax.dot_general(x, wg[j], dims, preferred_element_type=F32)
        up = lax.dot_general(x, wu[j], dims, preferred_element_type=F32)
        return (gate * jax.nn.sigmoid(gate) * up).astype(BF16)

    if nj == 1:
        act[...] = hidden_step(0)
    else:

        def body(j, carry):
            act[:, pl.ds(pl.multiple_of(j * hc, hc), hc)] = hidden_step(j)
            return carry

        lax.fori_loop(0, nj, body, 0)

    def pair_copy(src, dst, sems, dev):
        return pltpu.make_async_remote_copy(
            src_ref=src,
            dst_ref=dst,
            send_sem=sems.at[0],
            recv_sem=sems.at[1],
            device_id=dev,
            device_id_type=MESH,
        )

    copy_1 = [
        pair_copy(s1.at[k, 1 - core], r1.at[k], sem_1.at[k], core_dev) for k in range(nk)
    ]
    copy_2 = [pair_copy(s2.at[k, 1 - xbit], r2.at[k], sem_2.at[k], x_dev) for k in range(nk)]
    copy_3 = [
        [
            pair_copy(
                s3.at[k, lax.rem(quad + d, quads)], r3.at[k, quad], sem_3.at[k, d], quad_dev(d)
            )
            for d in range(1, quads)
        ]
        for k in range(nk)
    ]
    wait_3 = [
        [
            pair_copy(
                s3.at[k, lax.rem(quad + d, quads)],
                r3.at[k, lax.rem(quad + quads - d, quads)],
                sem_3.at[k, d],
                quad_dev(d),
            )
            for d in range(1, quads)
        ]
        for k in range(nk)
    ]

    def start_1(k):
        down_copy(k).wait()
        part[...] = jnp.dot(act[...], wd[k], preferred_element_type=F32)
        for b in range(n):
            s1[k, b % 2, b // 2] = part[b * tokens : (b + 1) * tokens, :].astype(BF16)
        copy_1[k].start()

    def start_2(k):
        copy_1[k].wait_recv()
        for q in range(quads):
            for y in range(2):
                h = q * 2 + y
                s2[k, y, q] = (s1[k, core, h].astype(F32) + r1[k, h].astype(F32)).astype(BF16)
        copy_2[k].start()

    def start_3(k):
        copy_2[k].wait_recv()
        for q in range(quads):
            s3[k, q] = (s2[k, xbit, q].astype(F32) + r2[k, q].astype(F32)).astype(BF16)
        r3[k, quad] = s3[k, quad]
        for copy in copy_3[k]:
            copy.start()

    token = lax.broadcasted_iota(jnp.int32, (tokens, 1), 0)
    margin = jnp.zeros((tokens, 1), F32)
    first = jnp.zeros((tokens, 1), jnp.int32)
    second = jnp.zeros((tokens, 1), jnp.int32)
    for t in range(new):
        for d in range(docs):
            here = token == t * docs + d
            margin = jnp.where(here, logits_ref[t, d, 0] - logits_ref[t, d, 1], margin)
            first = jnp.where(here, routes_ref[t, d, 0], first)
            second = jnp.where(here, routes_ref[t, d, 1], second)
    share_a = jax.nn.sigmoid(margin)
    share_b = 1.0 - share_a
    share = [
        jnp.where(first == e, share_a, 0.0) + jnp.where(second == e, share_b, 0.0)
        for e in range(EXPERTS)
    ]

    def finish(k):
        for copy in wait_3[k]:
            copy.wait_recv()
        lanes = slice(k * cw, (k + 1) * cw)
        acc = carried[:, lanes]
        for e in range(EXPERTS):
            per = quads // EXPERTS
            value = r3[k, e * per].astype(F32)
            for i in range(1, per):
                value = value + r3[k, e * per + i].astype(F32)
            acc = acc + share[e] * value
        for t in range(new):
            out_ref[t, :, lanes] = acc[t * docs : (t + 1) * docs].astype(out_ref.dtype)

    for step in range(nk + 3):
        if step < nk:
            start_1(step)
        if 0 <= step - 1 < nk:
            start_2(step - 1)
        if 0 <= step - 2 < nk:
            start_3(step - 2)
        if 0 <= step - 3 < nk:
            finish(step - 3)

    for copy in out_a + out_b + [c for pair in out_c for c in pair]:
        copy.wait_send()
    for k in range(nk):
        copy_1[k].wait_send()
        copy_2[k].wait_send()
        for copy in copy_3[k]:
            copy.wait_send()


def hidden_chunk(hidden):
    for size in range(256, 0, -16):
        if hidden % size == 0 and (size % 128 == 0 or size == hidden):
            return size
    return hidden


def per_device(
    hidden_in,
    norm_gain,
    queries,
    new_keys,
    new_values,
    cache_keys,
    cache_values,
    lengths,
    routes,
    gate_logits,
    w_gate,
    w_up,
    w_down,
):
    n = lax.axis_size("dp")
    new, docs, width = hidden_in.shape
    tokens = new * docs
    rows = n * tokens
    hidden = w_gate.shape[0]
    cache_len, kv_width = cache_keys.shape[1:]
    kv_heads = kv_width // HEAD_DIM
    hc = hidden_chunk(hidden)
    nj = hidden // hc
    nk = 4
    cw = width // nk
    quads = n // 4
    smem = pl.BlockSpec(memory_space=pltpu.SMEM)
    vmem = pl.BlockSpec(memory_space=pltpu.VMEM)
    hbm = pl.BlockSpec(memory_space=pl.ANY)
    dma = pltpu.SemaphoreType.DMA
    return pl.pallas_call(
        functools.partial(kernel, n, hc, cw),
        out_shape=jax.ShapeDtypeStruct(hidden_in.shape, BF16),
        in_specs=[smem] * 3 + [vmem] * 5 + [hbm] * 5,
        out_specs=vmem,
        scratch_shapes=[
            pltpu.VMEM(cache_keys.shape, BF16),
            pltpu.VMEM(cache_values.shape, BF16),
            pltpu.VMEM((nj, hc, width), BF16),
            pltpu.VMEM((nj, hc, width), BF16),
            pltpu.VMEM((nk, hidden, cw), BF16),
            pltpu.VMEM((docs * kv_heads, new * width // kv_width, HEAD_DIM), F32),
            pltpu.VMEM((tokens, width), F32),
            pltpu.VMEM((tokens, width), F32),
            pltpu.VMEM((n, tokens, width), BF16),
            pltpu.VMEM((rows, width), F32),
            pltpu.VMEM((rows, width), BF16),
            pltpu.VMEM((rows, hidden), BF16),
            pltpu.VMEM((rows, cw), F32),
            pltpu.VMEM((nk, 2, n // 2, tokens, cw), BF16),
            pltpu.VMEM((nk, n // 2, tokens, cw), BF16),
            pltpu.VMEM((nk, 2, quads, tokens, cw), BF16),
            pltpu.VMEM((nk, quads, tokens, cw), BF16),
            pltpu.VMEM((nk, quads, tokens, cw), BF16),
            pltpu.VMEM((nk, quads, tokens, cw), BF16),
            dma((2, docs)),
            dma((2, nj)),
            dma((nk,)),
            dma((2, quads)),
            dma((2, quads)),
            dma((2, 2, quads)),
            dma((nk, 2)),
            dma((nk, 2)),
            dma((nk, quads, 2)),
        ],
        compiler_params=pltpu.CompilerParams(
            collective_id=0, has_side_effects=True, vmem_limit_bytes=67043328
        ),
        name="decode_layer",
    )(
        lengths,
        routes,
        gate_logits,
        hidden_in,
        norm_gain.reshape(1, width),
        queries,
        new_keys,
        new_values,
        cache_keys,
        cache_values,
        w_gate,
        w_up,
        w_down,
    )


def solution(mesh):
    in_specs = (
        P(None, ("grp", "dp"), None),
        P(),
        P(None, ("grp", "dp"), None),
        P(None, ("grp", "dp"), None),
        P(None, ("grp", "dp"), None),
        P(("grp", "dp"), None, None),
        P(("grp", "dp"), None, None),
        P(("grp", "dp")),
        P(None, ("grp", "dp"), None),
        P(None, ("grp", "dp"), None),
        P("dp", None),
        P("dp", None),
        P("dp", None),
    )
    out_specs = P(None, ("grp", "dp"), None)
    return jax.shard_map(
        per_device, mesh=mesh, in_specs=in_specs, out_specs=out_specs, check_vma=False
    )
```

time: 75.9 us -> 58.2 us (0.77)
  Pallas kernels: 0 us -> 56.5 us
  matrix products: 26.1 us -> 0 us
  blocking collectives: 21.5 us -> 0 us
  waiting for transfers between devices: 13.9 us -> 0 us
  local copies, waits for them, and re-layouts: 6.33 us -> 1.4 us
  starting transfers between devices: 4.17 us -> 0 us
  other arithmetic: 3.07 us -> 0 us
    pallas_call x0 -> x1, Pallas kernels: none -> 56.5 us  [per_device(): pl.pallas_call(functools.partial(kernel, n, hc, cw), out_shape=jax.ShapeD...]
    dot_general x10 -> x0, matrix products: 26.1 us -> none  [the longest x1 13.5 us: expert_rows(): return jnp.dot(act, w_down, preferred_element_type=jnp.float32)]
    all_to_all x1 -> x0, blocking collectives: 21.5 us -> none  [per_device(): lax.all_to_all(payload, 'dp', split_axis=0, concat_axis=0, tiled=True)]
    all_to_all x1 -> x0, waiting for transfers between devices: 13.9 us -> none  [per_device(): lax.all_to_all(partial_value.astype(jnp.bfloat16), 'dp', split_axis=0, co...]
    all_to_all x1 -> x0, starting transfers between devices: 4.17 us -> none  [per_device(): lax.all_to_all(partial_value.astype(jnp.bfloat16), 'dp', split_axis=0, co...]
    unnamed x18 -> x1, local copies, waits for them, and re-layouts: 3.02 us -> 1.4 us
    reshape x13 -> x0, local copies, waits for them, and re-layouts: 1.54 us -> none  [the longest x1 0.79 us: attend(): query_heads = queries.reshape(NEW, docs, KV_HEADS, group_size, HEAD_DIM)]
    reduce_sum x6 -> x0, other arithmetic: 1.07 us -> none  [the longest x2 0.37 us: slot_table(): slot_ids = flat_ids * CAP + jnp.sum(before * matches, axis=1)]
  transfers between devices with their start and end apart: 1 -> 0, of which waited for: 1 -> 0; matrix products, arithmetic and copies ran while one was open for 0% -> 0% of each run, Pallas kernels for 0% -> 0%
where the time goes in v1:
time: 58.2 us; the launch traced here: 57.9 us
  Pallas kernels  56.5 us (97%)
  local copies, waits for them, and re-layouts  1.4 us (2%)
    pallas_call x1, Pallas kernels, per_device(): pl.pallas_call(functools.partial(kernel, n, hc, cw), out_shape=jax.ShapeD...  56.5 us
    unnamed x1, local copies, waits for them, and re-layouts  1.4 us

profile of v1, /device:TPU:0, one launch (start us, length us, event | category | flops | bytes accessed | tf_op | source)
XLA Modules:
  0.0 57.9 jit_solution(13626266246914388338)
XLA Ops:
  0.0 56.5 %decode_layer.1 = bf16[2,2,4096]{2,1,0:T(2,128)(2,1)} custom-call(s32[2]{0:T(128)} %lengths_ref.1, s32[2,2,2]{2,1,0:T(2,128)} %routes_ref.1, f32[2,2,2]{2,1,0:T(2,128)} %logits_ref.1, bf16[2,2,4096]{2,1,0:T(2,128)(2,1)} %hidden_ref.1, f32[1,4096]{1,0:T(1,128)} %bitcast.1, bf16[2,2,4096]{2,1,0:T(2,128)(2,1)} %q_ref.1, bf16[2,2,1024]{2,1,0:T(2,128)(2,1)} %nk_ref.1, ...), custom_call_target="tpu_custom_call" | custom-call | tf_op jit(solution)/shard_map/decode_layer/pallas_call | solution.py:402
  56.5 1.4 %copy.15 = bf16[2,2,4096]{2,1,0:T(2,128)(2,1)} copy(bf16[2,2,4096]{2,1,0:T(2,128)(2,1)} %decode_layer.1) | data formatting | bytes 65536

commit v2 on v1

--- a/solution.py
+++ b/solution.py
@@ -106,12 +106,6 @@
     def down_copy(k):
         return pltpu.make_async_copy(wd_hbm.at[:, pl.ds(k * cw, cw)], wd.at[k], sem_d.at[k])
 
-    for j in range(nj):
-        gate_copy(j).start()
-        up_copy(j).start()
-    for k in range(nk):
-        down_copy(k).start()
-
     for t in range(new):
         q32 = q_ref[t].astype(F32)
         for d in range(docs):
@@ -125,9 +119,14 @@
     nv32 = [nv_ref[u].astype(F32) for u in range(new)]
     row_pos = lax.broadcasted_iota(jnp.int32, (rows8, 1), 0) // group
     col = lax.broadcasted_iota(jnp.int32, (rows8, cache_len), 1)
+    for copy in k_copies + v_copies:
+        copy.wait()
+    for j in range(nj):
+        gate_copy(j).start()
+        up_copy(j).start()
+    for k in range(nk):
+        down_copy(k).start()
     for d in range(docs):
-        k_copies[d].wait()
-        v_copies[d].wait()
         keep = col < lengths_ref[d]
         for h in range(kv_heads):
             lanes = slice(h * HEAD_DIM, (h + 1) * HEAD_DIM)
@@ -392,7 +391,7 @@
     kv_heads = kv_width // HEAD_DIM
     hc = hidden_chunk(hidden)
     nj = hidden // hc
-    nk = 4
+    nk = 2
     cw = width // nk
     quads = n // 4
     smem = pl.BlockSpec(memory_space=pltpu.SMEM)

time: 58.2 us -> 43.9 us (0.75)
  Pallas kernels: 56.5 us -> 42.2 us
    pallas_call x1, Pallas kernels: 56.5 us -> 42.2 us  [per_device(): pl.pallas_call(functools.partial(kernel, n, hc, cw), out_shape=jax.ShapeD...]
where the time goes in v2:
time: 43.9 us; the launch traced here: 43.7 us
  Pallas kernels  42.2 us (96%)
  local copies, waits for them, and re-layouts  1.4 us (3%)
    pallas_call x1, Pallas kernels, per_device(): pl.pallas_call(functools.partial(kernel, n, hc, cw), out_shape=jax.ShapeD...  42.2 us
    unnamed x1, local copies, waits for them, and re-layouts  1.4 us

profile of v2, /device:TPU:0, one launch (start us, length us, event | category | flops | bytes accessed | tf_op | source)
XLA Modules:
  0.0 43.7 jit_solution(10137377853894691004)
XLA Ops:
  0.0 42.2 %decode_layer.1 = bf16[2,2,4096]{2,1,0:T(2,128)(2,1)} custom-call(s32[2]{0:T(128)} %lengths_ref.1, s32[2,2,2]{2,1,0:T(2,128)} %routes_ref.1, f32[2,2,2]{2,1,0:T(2,128)} %logits_ref.1, bf16[2,2,4096]{2,1,0:T(2,128)(2,1)} %hidden_ref.1, f32[1,4096]{1,0:T(1,128)} %bitcast.1, bf16[2,2,4096]{2,1,0:T(2,128)(2,1)} %q_ref.1, bf16[2,2,1024]{2,1,0:T(2,128)(2,1)} %nk_ref.1, ...), custom_call_target="tpu_custom_call" | custom-call | tf_op jit(solution)/shard_map/decode_layer/pallas_call | solution.py:401
  42.3 1.4 %copy.15 = bf16[2,2,4096]{2,1,0:T(2,128)(2,1)} copy(bf16[2,2,4096]{2,1,0:T(2,128)(2,1)} %decode_layer.1) | data formatting | bytes 65536
